TPU v7x, 8 devices: a whole 2x2x1 slice. The times are simulated.
8 devices in a mesh: dp: 2 (over z, y), sp: 4 (over x, core).
Axes of the slice: x: 2, y: 2, z: 1, core: 2. Of those that a mesh axis runs over, the one named last changes fastest.
Arguments:
- hidden: bfloat16 [4096, 5120], P(('dp', 'sp')), parts along dimension 0
- ln_gain: bfloat16 [5120], replicated
- w_q: bfloat16 [5120, 8192], replicated
- w_k: bfloat16 [5120, 1024], replicated
- w_v: bfloat16 [5120, 1024], replicated
- w_o: bfloat16 [8192, 5120], replicated
- q_gain: bfloat16 [128], replicated
- k_gain: bfloat16 [128], replicated
Outputs:
- output: bfloat16 [4096, 5120], P(('dp', 'sp')), parts along dimension 0
There are 2 independent parts. A program takes and returns all parts, laid end to end along the dimension named above; an argument that names none is the same for every part.
All inputs are finite; a program needn't handle non-finite values.
Results may differ from a plain program's by a relative error of at most 0.00696765.
Values are sent between devices in bfloat16 or wider.
A program may use at most 1 GiB of HBM per device.

v0:
```python
import jax
import jax.numpy as jnp
from jax import lax
from jax.sharding import PartitionSpec as P

EPS = 1e-6
THETA = 1000000.0


def head_norm(values, gain):
    return values * lax.rsqrt(jnp.mean(values * values, axis=-1, keepdims=True) + EPS) * gain.astype(jnp.float32)


def rotate(values, positions):
    head_dim = values.shape[-1]
    half = head_dim // 2
    inv_freq = jnp.power(THETA, -(jnp.arange(half, dtype=jnp.float32) * (2.0 / head_dim)))
    angles = positions.astype(jnp.float32)[:, None] * inv_freq[None, :]
    cos_pos = jnp.cos(angles)[:, None, :]
    sin_pos = jnp.sin(angles)[:, None, :]
    first_half = values[..., :half]
    second_half = values[..., half:]
    return jnp.concatenate([first_half * cos_pos - second_half * sin_pos, second_half * cos_pos + first_half * sin_pos], axis=-1)


def project(hidden, ln_gain, w_q, w_k, w_v, q_gain, k_gain, positions):
    tokens = hidden.shape[0]
    head_dim = q_gain.shape[0]
    hidden_f32 = hidden.astype(jnp.float32)
    normed = (hidden_f32 * lax.rsqrt(jnp.mean(hidden_f32 * hidden_f32, axis=-1, keepdims=True) + EPS) * ln_gain.astype(jnp.float32)).astype(jnp.bfloat16)
    q_raw = jnp.dot(normed, w_q, preferred_element_type=jnp.float32).reshape(tokens, -1, head_dim)
    k_raw = jnp.dot(normed, w_k, preferred_element_type=jnp.float32).reshape(tokens, -1, head_dim)
    v_local = jnp.dot(normed, w_v, preferred_element_type=jnp.float32).astype(jnp.bfloat16).reshape(tokens, -1, head_dim)
    q_local = rotate(head_norm(q_raw, q_gain), positions).astype(jnp.bfloat16)
    k_local = rotate(head_norm(k_raw, k_gain), positions).astype(jnp.bfloat16)
    return hidden_f32, q_local, k_local, v_local


def attend(q_all, k_all, v_all, q_start):
    q_rows, q_heads, head_dim = q_all.shape
    k_rows = k_all.shape[0]
    k_heads = k_all.shape[1]
    group = q_heads // k_heads
    limit = 2 ** 25 // (q_heads * k_rows)
    block_rows = min(q_rows, 2 ** max(3, min(9, limit.bit_length() - 1)))
    num_blocks = q_rows // block_rows
    q_blocks = q_all.reshape(num_blocks, block_rows, k_heads, group, head_dim)
    key_pos = jnp.arange(k_rows)
    score_scale = head_dim ** -0.5

    def one_block(block_args):
        q_block, block_idx = block_args
        scores = jnp.einsum('qkgd,skd->kgqs', q_block, k_all, preferred_element_type=jnp.float32) * score_scale
        q_pos = q_start + block_idx * block_rows + jnp.arange(block_rows)
        visible = q_pos[:, None] >= key_pos[None, :]
        scores = jnp.where(visible, scores, -jnp.inf)
        attn_prob = jax.nn.softmax(scores, axis=-1).astype(jnp.bfloat16)
        mixed = jnp.einsum('kgqs,skd->qkgd', attn_prob, v_all, preferred_element_type=jnp.float32)
        return mixed.astype(jnp.bfloat16)

    outputs = lax.map(one_block, (q_blocks, jnp.arange(num_blocks)))
    return outputs.reshape(q_rows, q_heads, head_dim)


def finish(hidden_f32, mixed, w_o):
    tokens = mixed.shape[0]
    result = hidden_f32 + jnp.dot(mixed.reshape(tokens, -1), w_o, preferred_element_type=jnp.float32)
    return result.astype(jnp.bfloat16)


def solution(mesh):
    group_size = mesh.shape['sp']

    def device_step(hidden, ln_gain, w_q, w_k, w_v, w_o, q_gain, k_gain):
        tokens = hidden.shape[0]
        head_dim = q_gain.shape[0]
        kv_heads = w_k.shape[1] // head_dim
        copies = max(1, group_size // kv_heads)
        positions = lax.axis_index('sp') * tokens + jnp.arange(tokens)
        hidden_f32, q_local, k_local, v_local = project(hidden, ln_gain, w_q, w_k, w_v, q_gain, k_gain, positions)
        q_heads = lax.all_to_all(q_local, 'sp', 1, 0, tiled=True)
        k_heads = lax.all_to_all(jnp.repeat(k_local, copies, axis=1), 'sp', 1, 0, tiled=True)
        v_heads = lax.all_to_all(jnp.repeat(v_local, copies, axis=1), 'sp', 1, 0, tiled=True)
        mixed = attend(q_heads, k_heads, v_heads, 0)
        mixed_local = lax.all_to_all(mixed, 'sp', 0, 1, tiled=True)
        return finish(hidden_f32, mixed_local, w_o)

    row_spec = P(('dp', 'sp'), None)
    return jax.shard_map(device_step, mesh=mesh, in_specs=(row_spec, P(), P(), P(), P(), P(), P(), P()), out_specs=row_spec, check_vma=False)
```

profile of v0, /device:TPU:3, one launch (start us, length us, event | category | flops | bytes accessed | tf_op | source)
XLA Modules:
  0.0 626.0 jit_solution(16026289572016212354)
XLA Ops:
  0.0 0.7 convert_element_type.41
  0.7 3.6 fusion.36
  4.3 0.0 copy-start.7
  4.4 9.9 %fusion.43 = f32[512,1024]{1,0:T(8,128)S(1)} fusion(bf16[5120,1024]{1,0:T(8,128)(2,1)} %param.13, bf16[512,5120]{1,0:T(8,128)(2,1)} %param.10, f32[5120]{0:T(1024)S(1)} %convert_element_type.41, f32[512]{0:T(512)S(1)} %add_rsqrt_fusion.2), kind=kOutput, calls=%fused_computation.58 | convolution fusion | flops 5379194880 | bytes 17848320 | tf_op jit(solution)/shard_map/dot_general | solution.py:32
  14.3 0.0 copy-done.5
  14.3 0.5 copy.50
  14.8 0.6 multiply_reduce_fusion.1
  15.4 0.1 copy.35
  15.5 0.0 copy-done.7
  15.5 1.0 multiply_cosine_fusion
  16.5 0.0 copy-start.1
  16.5 0.0 copy-start.3
  16.5 0.7 fusion.40
  17.2 0.8 subtract_convert_fusion.1
  18.0 0.0 copy-done.1
  18.0 0.0 copy-done.3
  18.0 1.5 pad_maximum_fusion.1
  19.6 3.7 all-to-all-start.1
  23.3 50.5 %fusion.45 = f32[512,8192]{1,0:T(8,128)S(1)} fusion(bf16[5120,8192]{1,0:T(8,128)(2,1)} %param.12, bf16[512,5120]{1,0:T(8,128)(2,1)} %param.10, f32[5120]{0:T(1024)} %copy-done.5, f32[512]{0:T(512)S(1)} %add_rsqrt_fusion.2), kind=kOutput, calls=%fused_computation.59 | convolution fusion | flops 42960158720 | bytes 105928704 | tf_op jit(solution)/shard_map/dot_general | solution.py:31
  73.8 0.0 copy-start
  73.8 3.8 copy.49
  77.6 1.9 copy-done
  79.5 4.7 multiply_reduce_fusion
  84.2 0.1 copy.33
  84.4 0.0 slice-start.1
  84.4 0.0 copy-start.6
  84.4 14.1 %fusion.35 = f32[512,64,128]{2,0,1:T(8,128)} fusion(f32[128]{0:T(128)S(1)} %convert_element_type.43, f32[512,64]{0,1:T(8,128)S(1)} %add_rsqrt_fusion, f32[512,8192]{1,0:T(8,128)} %copy-done), kind=kLoop, calls=%fused_computation.30 | loop fusion | flops 8388608 | bytes 33686016 | tf_op jit(solution)/shard_map/mul | solution.py:11
  98.5 0.0 copy-done.6
  98.5 8.6 %fusion.41 = bf16[64,8,8,128]{3,2,1,0:T(8,128)(2,1)S(1)} fusion(bf16[5120,1024]{1,0:T(8,128)(2,1)} %param.14, bf16[512,5120]{1,0:T(8,128)(2,1)S(1)} %bitcast.114, f32[5120]{0:T(1024)S(1)} %copy-done.6, f32[512]{0:T(512)S(1)} %add_rsqrt_fusion.2), kind=kOutput, calls=%fused_computation.48 | convolution fusion | flops 5379719168 | bytes 16799744 | tf_op jit(solution)/shard_map/dot_general | solution.py:33
  107.1 1.2 copy.55
  108.3 0.0 all-to-all-done.1
  108.3 3.6 all-to-all-start.2
  111.9 0.0 copy-done.2
  111.9 12.5 %subtract_convert_fusion = (bf16[512,64,64]{2,0,1:T(8,128)(2,1)S(1)}, bf16[512,64,64]{2,0,1:T(8,128)(2,1)S(1)}) fusion(f32[512,64,128]{2,0,1:T(8,128)} %fusion.35, f32[512,64]{1,0:T(8,128)S(1)} %copy-done.4, f32[512,64]{1,0:T(8,128)S(1)} %copy-done.2), kind=kLoop, calls=%fused_computation.32 | loop fusion | flops 16777216 | bytes 25427968 | tf_op jit(solution)/shard_map/convert.2
  124.4 6.2 pad_maximum_fusion
  130.6 0.0 all-to-all-done.2
  130.6 5.8 all-to-all-start
  136.4 0.1 copy.37
  136.5 0.1 copy.39
  136.6 91.0 %all-to-all-done = bf16[512,64,128]{2,0,1:T(8,128)(2,1)} async-done(((bf16[512,64,128]{2,0,1:T(8,128)(2,1)}), bf16[512,64,128]{2,0,1:T(8,128)(2,1)}, u32[]{:S(2)}, u32[]{:S(2)}) %all-to-all-start) | async-done | bytes 8388640 | tf_op jit(solution)/shard_map/all_to_all | solution.py:81
  227.6 231.3 %while.11 = (s32[]{:T(128)}, bf16[4,512,2,8,128]{4,3,2,1,0:T(8,128)(2,1)}, s32[4]{0:T(128)S(1)}, bf16[4,512,2,8,128]{4,1,3,2,0:T(8,128)(2,1)}, bf16[2048,2,128]{...) while((s32[]{:T(128)}, ...), condition=%wide.region_6.7_spmd.clone, body=%wide.region_3.6_spmd.clone.sunk | while | flops 8692697088 | bytes 146871408 | solution.py:61
  227.6 0.6 dynamic_slice.29
  228.9 0.7 iota_compare_fusion.2
  229.6 30.4 %fusion.73 = (f32[2,8,512]{2,1,0:T(8,128)S(1)}, f32[2,8,512,2048]{3,2,1,0:T(8,128)}) fusion(pred[512,2048]{1,0:T(8,128)(4,1)S(1)} %iota_compare_fusion.2, bf16[4,512,2,8,128]{4,1,3,2,0:T(8,128)(2,1)} %get-tuple-element.137, s32[]{:T(128)} %get-tuple-element.126, bf16[2048,2,128]{2,0,1:T(8,128)(2,1)S(1)} %get-tuple-element.138), kind=kOutput, calls=%fused_computation.60.clone.1 | convolution fusion | flops 4362078208 | bytes 71336448 | tf_op jit(solution)/shard_map/while/body/eval_jaxpr/sub | solution.py:57
  259.9 22.8 %convert_bitcast_fusion.2 = bf16[1,512,2,8,128]{4,1,3,2,0:T(8,128)(2,1)S(1)} fusion(f32[2,8,512,2048]{3,2,1,0:T(8,128)} %get-tuple-element.116, f32[2,8,512]{2,1,0:T(8,128)S(1)} %get-tuple-element.117, bf16[2048,2,128]{2,0,1:T(8,128)(2,1)S(1)} %get-tuple-element.139), kind=kOutput, calls=%fused_computation.18.clone.1 | convolution fusion | flops 4329570304 | bytes 70287360 | tf_op jit(solution)/shard_map/while/body/eval_jaxpr/kgqs,skd->qkgd/dot_general | solution.py:58
  282.7 2.7 copy_dynamic-update-slice_fusion.2
  285.4 0.6 dynamic_slice.29
  286.7 0.7 iota_compare_fusion.2
  287.4 30.4 %fusion.73 = (f32[2,8,512]{2,1,0:T(8,128)S(1)}, f32[2,8,512,2048]{3,2,1,0:T(8,128)}) fusion(pred[512,2048]{1,0:T(8,128)(4,1)S(1)} %iota_compare_fusion.2, bf16[4,512,2,8,128]{4,1,3,2,0:T(8,128)(2,1)} %get-tuple-element.137, s32[]{:T(128)} %get-tuple-element.126, bf16[2048,2,128]{2,0,1:T(8,128)(2,1)S(1)} %get-tuple-element.138), kind=kOutput, calls=%fused_computation.60.clone.1 | convolution fusion | flops 4362078208 | bytes 71336448 | tf_op jit(solution)/shard_map/while/body/eval_jaxpr/sub | solution.py:57
  317.7 22.8 %convert_bitcast_fusion.2 = bf16[1,512,2,8,128]{4,1,3,2,0:T(8,128)(2,1)S(1)} fusion(f32[2,8,512,2048]{3,2,1,0:T(8,128)} %get-tuple-element.116, f32[2,8,512]{2,1,0:T(8,128)S(1)} %get-tuple-element.117, bf16[2048,2,128]{2,0,1:T(8,128)(2,1)S(1)} %get-tuple-element.139), kind=kOutput, calls=%fused_computation.18.clone.1 | convolution fusion | flops 4329570304 | bytes 70287360 | tf_op jit(solution)/shard_map/while/body/eval_jaxpr/kgqs,skd->qkgd/dot_general | solution.py:58
  340.6 2.7 copy_dynamic-update-slice_fusion.2
  343.3 0.6 dynamic_slice.29
  344.6 0.7 iota_compare_fusion.2
  345.2 30.4 %fusion.73 = (f32[2,8,512]{2,1,0:T(8,128)S(1)}, f32[2,8,512,2048]{3,2,1,0:T(8,128)}) fusion(pred[512,2048]{1,0:T(8,128)(4,1)S(1)} %iota_compare_fusion.2, bf16[4,512,2,8,128]{4,1,3,2,0:T(8,128)(2,1)} %get-tuple-element.137, s32[]{:T(128)} %get-tuple-element.126, bf16[2048,2,128]{2,0,1:T(8,128)(2,1)S(1)} %get-tuple-element.138), kind=kOutput, calls=%fused_computation.60.clone.1 | convolution fusion | flops 4362078208 | bytes 71336448 | tf_op jit(solution)/shard_map/while/body/eval_jaxpr/sub | solution.py:57
  375.6 22.8 %convert_bitcast_fusion.2 = bf16[1,512,2,8,128]{4,1,3,2,0:T(8,128)(2,1)S(1)} fusion(f32[2,8,512,2048]{3,2,1,0:T(8,128)} %get-tuple-element.116, f32[2,8,512]{2,1,0:T(8,128)S(1)} %get-tuple-element.117, bf16[2048,2,128]{2,0,1:T(8,128)(2,1)S(1)} %get-tuple-element.139), kind=kOutput, calls=%fused_computation.18.clone.1 | convolution fusion | flops 4329570304 | bytes 70287360 | tf_op jit(solution)/shard_map/while/body/eval_jaxpr/kgqs,skd->qkgd/dot_general | solution.py:58
  398.4 2.7 copy_dynamic-update-slice_fusion.2
  401.1 0.6 dynamic_slice.29
  402.4 0.7 iota_compare_fusion.2
  403.1 30.4 %fusion.73 = (f32[2,8,512]{2,1,0:T(8,128)S(1)}, f32[2,8,512,2048]{3,2,1,0:T(8,128)}) fusion(pred[512,2048]{1,0:T(8,128)(4,1)S(1)} %iota_compare_fusion.2, bf16[4,512,2,8,128]{4,1,3,2,0:T(8,128)(2,1)} %get-tuple-element.137, s32[]{:T(128)} %get-tuple-element.126, bf16[2048,2,128]{2,0,1:T(8,128)(2,1)S(1)} %get-tuple-element.138), kind=kOutput, calls=%fused_computation.60.clone.1 | convolution fusion | flops 4362078208 | bytes 71336448 | tf_op jit(solution)/shard_map/while/body/eval_jaxpr/sub | solution.py:57
  433.4 22.8 %convert_bitcast_fusion.2 = bf16[1,512,2,8,128]{4,1,3,2,0:T(8,128)(2,1)S(1)} fusion(f32[2,8,512,2048]{3,2,1,0:T(8,128)} %get-tuple-element.116, f32[2,8,512]{2,1,0:T(8,128)S(1)} %get-tuple-element.117, bf16[2048,2,128]{2,0,1:T(8,128)(2,1)S(1)} %get-tuple-element.139), kind=kOutput, calls=%fused_computation.18.clone.1 | convolution fusion | flops 4329570304 | bytes 70287360 | tf_op jit(solution)/shard_map/while/body/eval_jaxpr/kgqs,skd->qkgd/dot_general | solution.py:58
  456.2 2.7 copy_dynamic-update-slice_fusion.2
  458.9 99.6 %all_to_all.66 = bf16[2048,16,128]{2,1,0:T(8,128)(2,1)} all-to-all(bf16[2048,16,128]{2,1,0:T(8,128)(2,1)} %bitcast.109), channel_id=1, replica_groups=mesh['dp'=2,'sp'=4] {'sp'}, dimensions={0} | all-to-all | bytes 16777216 | tf_op jit(solution)/shard_map/all_to_all | solution.py:85
  558.5 13.8 %copy.41 = bf16[4,512,16,128]{1,3,2,0:T(8,128)(2,1)} copy(bf16[4,512,16,128]{3,2,1,0:T(8,128)(2,1)} %bitcast.108) | data formatting | bytes 16777216 | tf_op jit(solution)/shard_map/all_to_all | solution.py:85
  572.2 53.8 %fusion.39 = bf16[512,5120]{1,0:T(8,128)(2,1)} fusion(bf16[512,5120]{1,0:T(8,128)(2,1)} %param.10, bf16[512,8192]{0,1:T(8,128)(2,1)} %bitcast.110, bf16[8192,5120]{1,0:T(8,128)(2,1)} %param.15), kind=kOutput, calls=%fused_computation.40 | convolution fusion | flops 42957537280 | bytes 102760448 | tf_op jit(solution)/shard_map/dot_general | solution.py:67
  (23 shorter events, 0.1 us)
Async XLA Ops:
  0.7 13.6 %copy-start.5 = (f32[5120]{0:T(1024)}, f32[5120]{0:T(1024)S(1)}, u32[]{:S(2)}) copy-start(f32[5120]{0:T(1024)S(1)} %convert_element_type.41) | copy-start | bytes 61444
  4.3 11.2 %copy-start.7 = (bf16[128]{0:T(256)(128)(2,1)S(1)}, bf16[128]{0:T(256)(128)(2,1)}, u32[]{:S(2)}) copy-start(bf16[128]{0:T(256)(128)(2,1)} %param.17) | copy-start | bytes 772
  16.5 1.5 copy-start.1
  16.5 1.5 copy-start.3
  19.6 88.7 %all-to-all-start.1 = ((bf16[512,8,128]{2,0,1:T(8,128)(2,1)}), bf16[512,8,128]{2,0,1:T(8,128)(2,1)S(1)}, u32[]{:S(2)}, u32[]{:S(2)}) async-start(bf16[512,8,128]{2,0,1:T(8,128)(2,1)} %pad_maximum_fusion.1), calls=%async_computation.1 | async-start | bytes 2097152 | tf_op jit(solution)/shard_map/all_to_all | solution.py:82
  73.8 5.7 copy-start
  79.5 4.8 copy-start.8
  79.5 18.9 %slice-start = ((s8[5242880]{0:T(1024)(128)(4,1)}), s8[1048576]{0:T(1024)(128)(4,1)S(1)}, s32[]{:S(2)}) async-start(s8[5242880]{0:T(1024)(128)(4,1)} %bitcast.113), calls=%async_computation.4 | async-start | bytes 2097152
  84.4 14.1 %slice-start.1 = ((s8[5242880]{0:T(1024)(128)(4,1)}), s8[4194304]{0:T(1024)(128)(4,1)S(1)}, s32[]{:S(2)}) async-start(s8[5242880]{0:T(1024)(128)(4,1)} %bitcast.113), calls=%async_computation.5 | async-start | bytes 8388608
  84.4 14.1 %copy-start.6 = (f32[5120]{0:T(1024)S(1)}, f32[5120]{0:T(1024)}, u32[]{:S(2)}) copy-start(f32[5120]{0:T(1024)} %copy-done.5) | copy-start | bytes 61444
  98.5 13.4 %copy-start.2 = (f32[512,64]{1,0:T(8,128)S(1)}, f32[512,64]{1,0:T(8,128)}, u32[]{:S(2)}) copy-start(f32[512,64]{1,0:T(8,128)} %copy-done.1) | copy-start | bytes 393220
  98.5 13.4 %copy-start.4 = (f32[512,64]{1,0:T(8,128)S(1)}, f32[512,64]{1,0:T(8,128)}, u32[]{:S(2)}) copy-start(f32[512,64]{1,0:T(8,128)} %copy-done.3) | copy-start | bytes 393220
  108.3 22.3 %all-to-all-start.2 = ((bf16[512,8,128]{2,0,1:T(8,128)(2,1)}), bf16[512,8,128]{2,0,1:T(8,128)(2,1)S(1)}, u32[]{:S(2)}, u32[]{:S(2)}) async-start(bf16[512,8,128]{2,0,1:T(8,128)(2,1)} %bitcast.93), calls=%async_computation.2 | async-start | bytes 2097152 | tf_op jit(solution)/shard_map/all_to_all | solution.py:83
  130.6 97.0 %all-to-all-start = ((bf16[512,64,128]{2,0,1:T(8,128)(2,1)}), bf16[512,64,128]{2,0,1:T(8,128)(2,1)}, u32[]{:S(2)}, u32[]{:S(2)}) async-start(bf16[512,64,128]{2,0,1:T(8,128)(2,1)} %pad_maximum_fusion), calls=%async_computation | async-start | bytes 16777216 | tf_op jit(solution)/shard_map/all_to_all | solution.py:81
where the time goes:
time: 630 us; the launch traced here: 626 us
  matrix products  335 us (53%)
  blocking collectives  99.6 us (16%)
  waiting for transfers between devices  91 us (14%)
  other arithmetic  49 us (8%)
  local copies, waits for them, and re-layouts  34.8 us (6%)
  starting transfers between devices  13.1 us (2%)
    sub x4, matrix products, one_block(): attn_prob = jax.nn.softmax(scores, axis=-1).astype(jnp.bfloat16)  121 us
    all_to_all x1, blocking collectives, device_step(): mixed_local = lax.all_to_all(mixed, 'sp', 0, 1, tiled=True)  99.6 us
    dot_general x4, matrix products, one_block(): jnp.einsum('kgqs,skd->qkgd', attn_prob, v_all, preferred_element_type=jnp...  91.2 us
    all_to_all x1, waiting for transfers between devices, device_step(): q_heads = lax.all_to_all(q_local, 'sp', 1, 0, tiled=True)  91 us
    dot_general x1, matrix products, finish(): jnp.dot(mixed.reshape(tokens, -1), w_o, preferred_element_type=jnp.float32)  53.8 us
    dot_general x1, matrix products, project(): jnp.dot(normed, w_q, preferred_element_type=jnp.float32)  50.5 us
    mul x2, other arithmetic, head_norm(): values * lax.rsqrt(jnp.mean(values * values, axis=-1, keepdims=True) + EPS)  14.8 us
    all_to_all x1, local copies, waits for them, and re-layouts, device_step(): mixed_local = lax.all_to_all(mixed, 'sp', 0, 1, tiled=True)  13.8 us
  transfers between devices with their start and end apart: 3, of which 1 were waited for; matrix products, arithmetic and copies ran while one was open for 16% of the time, Pallas kernels for 0%

commit v1 on v0

v1 whole, which is shorter than its diff:
```python
import functools
import math

import jax
import jax.numpy as jnp
from jax import lax
from jax.experimental import pallas as pl
from jax.experimental.pallas import tpu as pltpu
from jax.sharding import PartitionSpec as P

EPS = 1e-6
THETA = 1000000.0
HD = 128
VMEM_LIMIT = 60 * 1024 * 1024
NT = (((1,), (1,)), ((), ()))
F32 = jnp.float32
BF16 = jnp.bfloat16
ANY = pl.BlockSpec(memory_space=pl.ANY)


def rope_tables(positions, gain):
    half = HD // 2
    inv_freq = jnp.power(THETA, -(jnp.arange(half, dtype=F32) * (2.0 / HD)))
    angles = positions.astype(F32)[:, None] * inv_freq[None, :]
    cos = jnp.cos(angles)
    sin = jnp.sin(angles)
    gain = gain.astype(F32)
    swapped = jnp.concatenate([gain[half:], gain[:half]])
    cos_g = jnp.concatenate([cos, cos], axis=1) * gain[None, :]
    sin_g = jnp.concatenate([-sin, sin], axis=1) * swapped[None, :]
    return cos_g, sin_g


def norm_rope(acc, cos_g, sin_g):
    var = jnp.mean(acc * acc, axis=-1, keepdims=True)
    n = acc * lax.rsqrt(var + EPS)
    return (n * cos_g + pltpu.roll(n, HD // 2, 1) * sin_g).astype(BF16)


def kv_kernel(meta, h_ref, wk_ref, wv_ref, cos_ref, sin_ref, own_ref, other_ref):
    n = pl.program_id(0)
    k = jnp.dot(h_ref[...], wk_ref[...], preferred_element_type=F32)
    v = jnp.dot(h_ref[...], wv_ref[...], preferred_element_type=F32)
    cos_g = cos_ref[...]
    sin_g = sin_ref[...]

    def put(out_ref, base):
        for i in range(2):
            cols = slice(i * HD, (i + 1) * HD)
            out_ref[0, base + i] = norm_rope(k[:, cols], cos_g, sin_g)
            out_ref[1, base + i] = v[:, cols].astype(BF16)

    for step in range(4):
        @pl.when(n == step)
        def _():
            put(own_ref if step < 2 else other_ref, (step % 2) * 2)


def kv_project(core, h, w_k, w_v, cos_g, sin_g):
    rows, dim = h.shape
    meta = jnp.stack([core]).astype(jnp.int32)
    wspec = pl.BlockSpec((dim, 256), lambda n, m: (0, (n + 2 * m[0]) % 4))
    full = lambda *s: pl.BlockSpec(s, lambda n, m: (0,) * len(s), pipeline_mode=pl.Buffered(1))
    out = jax.ShapeDtypeStruct((2, 4, rows, HD), BF16)
    return pl.pallas_call(
        kv_kernel,
        grid_spec=pltpu.PrefetchScalarGridSpec(
            num_scalar_prefetch=1,
            grid=(4,),
            in_specs=[full(rows, dim), wspec, wspec, full(rows, HD), full(rows, HD)],
            out_specs=[full(2, 4, rows, HD), full(2, 4, rows, HD)],
        ),
        out_shape=[out, out],
        compiler_params=pltpu.CompilerParams(vmem_limit_bytes=VMEM_LIMIT),
        cost_estimate=pl.CostEstimate(flops=4 * rows * dim * 1024, bytes_accessed=4 * dim * 1024, transcendentals=0),
        name='kv_proj',
    )(meta, h, w_k, w_v, cos_g, sin_g)


def q_kernel(meta, own_hbm, part_hbm, w_ref, cos_ref, sin_ref, q_ref, h_scr, sems):
    n = pl.program_id(0)
    core = meta[0]
    rows = own_hbm.shape[0]
    mine = pltpu.make_async_copy(own_hbm, h_scr.at[pl.ds(pl.multiple_of(core * rows, rows), rows)], sems.at[0])
    theirs = pltpu.make_async_copy(part_hbm, h_scr.at[pl.ds(pl.multiple_of((1 - core) * rows, rows), rows)], sems.at[1])

    @pl.when(n == 0)
    def _():
        mine.start()
        theirs.start()
        mine.wait()
        theirs.wait()

    heads = w_ref.shape[1] // HD
    for lo in range(0, 2 * rows, 512):
        r = slice(lo, lo + 512)
        acc = jnp.dot(h_scr[r, :], w_ref[...], preferred_element_type=F32)
        for i in range(heads):
            q_ref[i, r, :] = norm_rope(acc[:, i * HD:(i + 1) * HD], cos_ref[r, :], sin_ref[r, :])


def q_project(core, h_own, h_part, w_q, cos_g, sin_g):
    rows, dim = h_own.shape
    bn = 256
    steps = w_q.shape[1] // 2 // bn
    meta = jnp.stack([core]).astype(jnp.int32)
    full = lambda *s: pl.BlockSpec(s, lambda n, m: (0,) * len(s), pipeline_mode=pl.Buffered(1))
    return pl.pallas_call(
        q_kernel,
        grid_spec=pltpu.PrefetchScalarGridSpec(
            num_scalar_prefetch=1,
            grid=(steps,),
            in_specs=[ANY, ANY, pl.BlockSpec((dim, bn), lambda n, m: (0, n + steps * m[0])), full(2 * rows, HD), full(2 * rows, HD)],
            out_specs=pl.BlockSpec((bn // HD, 2 * rows, HD), lambda n, m: (n, 0, 0)),
            scratch_shapes=[pltpu.VMEM((2 * rows, dim), BF16), pltpu.SemaphoreType.DMA((2,))],
        ),
        out_shape=jax.ShapeDtypeStruct((steps * bn // HD, 2 * rows, HD), BF16),
        compiler_params=pltpu.CompilerParams(vmem_limit_bytes=VMEM_LIMIT),
        cost_estimate=pl.CostEstimate(flops=4 * rows * dim * bn * steps, bytes_accessed=2 * dim * bn * steps, transcendentals=0),
        name='q_proj',
    )(meta, h_own, h_part, w_q, cos_g, sin_g)


TILE = 128
KB = 512


def attn_kernel(meta, q_ref, own_hbm, part_hbm, same_hbm, cross_hbm, keep_ref, send_ref, k_scr, v_scr, s_scr, m_scr, acc_scr, sems):
    g = pl.program_id(0)
    t = pl.program_id(1)
    chip = meta[0]
    core = meta[1]
    rows = own_hbm.shape[2]
    group = q_ref.shape[0]
    scale = HD ** -0.5 * math.log2(math.e)

    def pieces(c, x):
        own_at = x * 2 * rows + c * rows
        part_at = x * 2 * rows + (1 - c) * rows
        copies = []
        for i, scr in enumerate((k_scr, v_scr)):
            copies.append((own_hbm, i, scr, own_at))
            copies.append((part_hbm, i, scr, part_at))
            if x == 1:
                copies.append((same_hbm, i, scr, c * rows))
                copies.append((cross_hbm, i, scr, (1 - c) * rows))
        return [pltpu.make_async_copy(src.at[i], dst.at[:, pl.ds(at, rows)], sems.at[j]) for j, (src, i, dst, at) in enumerate(copies)]

    @pl.when(jnp.logical_and(g == 0, t == 0))
    def _():
        for x in range(2):
            for c in range(2):
                @pl.when(jnp.logical_and(chip == x, core == c))
                def _():
                    cps = pieces(c, x)
                    for cp in cps:
                        cp.start()
                    for cp in cps:
                        cp.wait()

    pos0 = chip * 2 * rows + t * TILE
    nfull = pos0 // KB
    m_rows = group * TILE
    q = q_ref[...].reshape(m_rows, HD)

    def score(j):
        kb = k_scr[g, pl.ds(pl.multiple_of(j * KB, KB), KB), :]
        return lax.dot_general(q, kb, NT, preferred_element_type=F32)

    def lane_max(s):
        m = s[:, :HD]
        for i in range(1, KB // HD):
            m = jnp.maximum(m, s[:, i * HD:(i + 1) * HD])
        return m

    s = score(nfull)
    off = pos0 - nfull * KB
    row = lax.broadcasted_iota(jnp.int32, (group, TILE, KB), 1).reshape(m_rows, KB) + off
    col = lax.broadcasted_iota(jnp.int32, (m_rows, KB), 1)
    s = jnp.where(row >= col, s, -jnp.inf)
    s_scr[nfull] = s
    m_scr[...] = lane_max(s)

    def first(j, _):
        s = score(j)
        s_scr[j] = s
        m_scr[...] = jnp.maximum(m_scr[...], lane_max(s))
        return 0

    lax.fori_loop(0, nfull, first, 0)
    m = jnp.max(m_scr[...], axis=1, keepdims=True) * scale
    m_scr[...] = jnp.broadcast_to(m, m_scr.shape)
    acc_scr[...] = jnp.zeros_like(acc_scr)

    def second(j, _):
        m = m_scr[:, :1]
        p = jnp.exp2(s_scr[j] * scale - m).astype(BF16)
        vb = v_scr[g, pl.ds(pl.multiple_of(j * KB, KB), KB), :]
        ve = jnp.concatenate([vb, jnp.ones((KB, HD), BF16)], axis=1)
        acc_scr[...] += jnp.dot(p, ve, preferred_element_type=F32)
        return 0

    lax.fori_loop(0, nfull + 1, second, 0)
    acc = acc_scr[...]
    o = (acc[:, :HD] / acc[:, HD:]).astype(BF16).reshape(group, TILE, HD)
    per = rows // TILE
    at = pl.ds(pl.multiple_of((t % per) * TILE, TILE), TILE)

    @pl.when(t // per == core)
    def _():
        for i in range(group):
            keep_ref[at, i * HD:(i + 1) * HD] = o[i]

    @pl.when(t // per != core)
    def _():
        for i in range(group):
            send_ref[at, i * HD:(i + 1) * HD] = o[i]


def attention(chip, core, q, kv_own, kv_part, kv_same, kv_cross):
    heads, q_rows, _ = q.shape
    rows = q_rows // 2
    seq = 4 * rows
    group = 8
    meta = jnp.stack([chip, core]).astype(jnp.int32)
    out = jax.ShapeDtypeStruct((rows, heads * HD), BF16)
    ospec = pl.BlockSpec((rows, group * HD), lambda g, t, m: (0, g))
    return pl.pallas_call(
        attn_kernel,
        grid_spec=pltpu.PrefetchScalarGridSpec(
            num_scalar_prefetch=1,
            grid=(heads // group, q_rows // TILE),
            in_specs=[pl.BlockSpec((group, TILE, HD), lambda g, t, m: (g, t, 0)), ANY, ANY, ANY, ANY],
            out_specs=[ospec, ospec],
            scratch_shapes=[
                pltpu.VMEM((heads // group, seq, HD), BF16),
                pltpu.VMEM((heads // group, seq, HD), BF16),
                pltpu.VMEM((seq // KB, group * TILE, KB), F32),
                pltpu.VMEM((group * TILE, HD), F32),
                pltpu.VMEM((group * TILE, 2 * HD), F32),
                pltpu.SemaphoreType.DMA((8,)),
            ],
        ),
        out_shape=[out, out],
        compiler_params=pltpu.CompilerParams(vmem_limit_bytes=VMEM_LIMIT),
        cost_estimate=pl.CostEstimate(flops=4 * heads * q_rows * seq * HD, bytes_accessed=6 * heads * q_rows * HD, transcendentals=0),
        name='attn',
    )(meta, q, kv_own, kv_part, kv_same, kv_cross)


def out_kernel(meta, keep_ref, recv_ref, wa_ref, wb_ref, x_ref, o_ref):
    acc = jnp.dot(keep_ref[...], wa_ref[...], preferred_element_type=F32)
    acc += jnp.dot(recv_ref[...], wb_ref[...], preferred_element_type=F32)
    o_ref[...] = (acc + x_ref[...].astype(F32)).astype(BF16)


def out_project(core, keep, recv, w_o, x):
    rows, half = keep.shape
    dim = w_o.shape[1]
    bn = 256
    meta = jnp.stack([core]).astype(jnp.int32)
    full = pl.BlockSpec((rows, half), lambda n, m: (0, 0), pipeline_mode=pl.Buffered(1))
    tile = pl.BlockSpec((rows, bn), lambda n, m: (0, n))
    return pl.pallas_call(
        out_kernel,
        grid_spec=pltpu.PrefetchScalarGridSpec(
            num_scalar_prefetch=1,
            grid=(dim // bn,),
            in_specs=[full, full, pl.BlockSpec((half, bn), lambda n, m: (m[0], n)), pl.BlockSpec((half, bn), lambda n, m: (1 - m[0], n)), tile],
            out_specs=tile,
        ),
        out_shape=jax.ShapeDtypeStruct((rows, dim), BF16),
        compiler_params=pltpu.CompilerParams(vmem_limit_bytes=VMEM_LIMIT),
        cost_estimate=pl.CostEstimate(flops=4 * rows * half * dim, bytes_accessed=4 * half * dim, transcendentals=0),
        name='out_proj',
    )(meta, keep, recv, w_o, w_o, x)


PARTNER = [(0, 1), (1, 0), (2, 3), (3, 2)]


def solution(mesh):
    def device_step(hidden, ln_gain, w_q, w_k, w_v, w_o, q_gain, k_gain):
        rows = hidden.shape[0]
        sp = lax.axis_index('sp')
        chip = sp // 2
        core = sp % 2
        x = hidden.astype(F32)
        h = (x * lax.rsqrt(jnp.mean(x * x, axis=-1, keepdims=True) + EPS) * ln_gain.astype(F32)).astype(BF16)
        h_part = lax.ppermute(h, 'sp', PARTNER)
        cos_k, sin_k = rope_tables(sp * rows + jnp.arange(rows), k_gain)
        cos_q, sin_q = rope_tables(chip * 2 * rows + jnp.arange(2 * rows), q_gain)
        kv_own, kv_other = kv_project(core, h, w_k, w_v, cos_k, sin_k)
        kv_part = lax.ppermute(kv_other, 'sp', PARTNER)
        kv_same = lax.ppermute(kv_own, 'sp', [(0, 2), (1, 3)])
        kv_cross = lax.ppermute(kv_other, 'sp', [(0, 3), (1, 2)])
        q = q_project(core, h, h_part, w_q, cos_q, sin_q)
        keep, send = attention(chip, core, q, kv_own, kv_part, kv_same, kv_cross)
        recv = lax.ppermute(send, 'sp', PARTNER)
        return out_project(core, keep, recv, w_o, hidden)

    row_spec = P(('dp', 'sp'), None)
    return jax.shard_map(device_step, mesh=mesh, in_specs=(row_spec, P(), P(), P(), P(), P(), P(), P()), out_specs=row_spec, check_vma=False)
```

time: 630 us -> 306 us (0.49)
  matrix products: 335 us -> 0 us
  Pallas kernels: 0 us -> 275 us
  blocking collectives: 99.6 us -> 0 us
  waiting for transfers between devices: 91 us -> 6.8 us
  local copies, waits for them, and re-layouts: 34.8 us -> 2.42 us
  other arithmetic: 49 us -> 17.2 us
  starting transfers between devices: 13.1 us -> 3.96 us
    pallas_call x0 -> x4, Pallas kernels: none -> 275 us  [the longest x1 128 us: attention(): pl.pallas_call(attn_kernel, grid_spec=pltpu.PrefetchScalarGridSpec(num_sc...]
    dot_general x8 -> x0, matrix products: 214 us -> none  [the longest x4 91.2 us: one_block(): jnp.einsum('kgqs,skd->qkgd', attn_prob, v_all, preferred_element_type=jnp...]
    sub x4 -> x0, matrix products: 121 us -> none  [one_block(): attn_prob = jax.nn.softmax(scores, axis=-1).astype(jnp.bfloat16)]
    all_to_all x1 -> x0, blocking collectives: 99.6 us -> none  [device_step(): mixed_local = lax.all_to_all(mixed, 'sp', 0, 1, tiled=True)]
    all_to_all x3 -> x0, waiting for transfers between devices: 91 us -> none  [the longest x1 91 us: device_step(): q_heads = lax.all_to_all(q_local, 'sp', 1, 0, tiled=True)]
    all_to_all x3 -> x0, local copies, waits for them, and re-layouts: 13.9 us -> none  [the longest x1 13.8 us: device_step(): mixed_local = lax.all_to_all(mixed, 'sp', 0, 1, tiled=True)]
    all_to_all x3 -> x0, starting transfers between devices: 13.1 us -> none  [the longest x1 5.85 us: device_step(): q_heads = lax.all_to_all(q_local, 'sp', 1, 0, tiled=True)]
    another operation x2 -> x1, other arithmetic: 13.3 us -> 0.65 us  [attention(): meta = jnp.stack([chip, core]).astype(jnp.int32)]
  transfers between devices with their start and end apart: 3 -> 5, of which waited for: 1 -> 1; matrix products, arithmetic and copies ran while one was open for 16% -> 2% of each run, Pallas kernels for 0% -> 31%
where the time goes in v1:
time: 306 us
  Pallas kernels  275 us (90%)
  other arithmetic  17.2 us (6%)
  waiting for transfers between devices  6.8 us (2%)
  starting transfers between devices  3.96 us (1%)
    pallas_call x1, Pallas kernels, attention(): pl.pallas_call(attn_kernel, grid_spec=pltpu.PrefetchScalarGridSpec(num_sc...  128 us
    pallas_call x1, Pallas kernels, q_project(): pl.pallas_call(q_kernel, grid_spec=pltpu.PrefetchScalarGridSpec(num_scala...  74.9 us
    pallas_call x1, Pallas kernels, out_project(): pl.pallas_call(out_kernel, grid_spec=pltpu.PrefetchScalarGridSpec(num_sca...  53.7 us
    pallas_call x1, Pallas kernels, kv_project(): pl.pallas_call(kv_kernel, grid_spec=pltpu.PrefetchScalarGridSpec(num_scal...  19 us
    convert_element_type x1, other arithmetic, device_step(): (x * lax.rsqrt(jnp.mean(x * x, axis=-1, keepdims=True) + EPS) * ln_gain.a...  6.8 us
    ppermute x1, waiting for transfers between devices, device_step(): recv = lax.ppermute(send, 'sp', PARTNER)  6.79 us
  transfers between devices with their start and end apart: 5, of which 1 were waited for; matrix products, arithmetic and copies ran while one was open for 2% of the time, Pallas kernels for 31%

profile of v1, /device:TPU:3, one launch (start us, length us, event | category | flops | bytes accessed | tf_op | source)
XLA Modules:
  0.0 305.8 jit_solution(17379869708906416709)
XLA Ops:
  0.0 0.0 copy-start
  0.0 0.7 convert_element_type.30
  0.7 3.6 %fusion = f32[512]{0:T(512)S(1)} fusion(bf16[512,5120]{1,0:T(8,128)(2,1)} %x_ref.1), kind=kLoop, calls=%fused_computation.2 | loop fusion | flops 7863808 | bytes 5244928 | tf_op jit(solution)/shard_map/reduce_sum | solution.py:289
  4.3 6.8 %fusion.2.own_hbm.h_ref = bf16[512,5120]{1,0:T(8,128)(2,1)} fusion(bf16[512,5120]{1,0:T(8,128)(2,1)} %x_ref.1, f32[5120]{0:T(1024)S(1)} %convert_element_type.30, f32[512]{0:T(512)S(1)} %add_rsqrt_fusion), kind=kLoop, calls=%fused_computation.4 | loop fusion | flops 10485760 | bytes 10508288 | tf_op jit(solution)/shard_map/convert_element_type | solution.py:289
  11.1 0.7 collective-permute-start
  11.8 0.0 copy-done
  11.8 0.1 fusion.5
  11.9 0.1 pad_maximum_fusion.1
  12.0 1.0 fusion.4
  13.0 1.0 maximum_multiply_fusion.2
  14.0 0.0 copy-start.1
  14.0 19.0 %kv_proj.1 = (bf16[2,4,512,128]{3,2,1,0:T(8,128)(2,1)}, bf16[2,4,512,128]{3,2,1,0:T(8,128)(2,1)}) custom-call(s32[1]{0:T(128)} %bitcast.meta, bf16[512,5120]{1,0:T(8,128)(2,1)} %fusion.2.own_hbm.h_ref, bf16[5120,1024]{1,0:T(8,128)(2,1)} %wk_ref.1, bf16[5120,1024]{1,0:T(8,128)(2,1)} %wv_ref.1, f32[512,128]{1,0:T(8,128)} %get-tuple-element.25.cos_ref, ...), custom_call_target="tpu_custom_call" | custom-call | flops 10737418240 | bytes 20971520 | tf_op jit(solution)/shard_map/kv_proj/pallas_call | solution.py:65
  32.9 0.1 collective-permute-start.1
  33.0 1.3 collective-permute-start.3
  34.3 1.5 collective-permute-start.2
  35.8 0.0 copy-done.1
  35.8 0.6 pad_add_fusion.meta
  36.4 0.1 fusion.6
  36.5 0.1 pad_maximum_fusion
  36.6 1.9 fusion.3
  38.5 1.3 maximum_multiply_fusion
  39.8 0.0 collective-permute-done.part_hbm
  39.8 74.9 %q_proj.1.q_ref = bf16[32,1024,128]{2,1,0:T(8,128)(2,1)} custom-call(s32[1]{0:T(128)} %bitcast.meta, bf16[512,5120]{1,0:T(8,128)(2,1)} %fusion.2.own_hbm.h_ref, bf16[512,5120]{1,0:T(8,128)(2,1)} %collective-permute-done.part_hbm, bf16[5120,8192]{1,0:T(8,128)(2,1)} %w_ref.1, f32[1024,128]{1,0:T(8,128)} %get-tuple-element.23.cos_ref, ...), custom_call_target="tpu_custom_call" | custom-call | flops 42949672960 | bytes 41943040 | tf_op jit(solution)/shard_map/q_proj/pallas_call | solution.py:108
  114.7 0.0 collective-permute-done.1.part_hbm
  114.7 0.0 copy-start.2
  114.7 0.0 collective-permute-done.2.same_hbm
  114.7 0.0 copy-start.4
  114.7 0.0 collective-permute-done.3.cross_hbm
  114.7 1.0 copy-done.2
  115.8 0.3 copy-done.4
  116.0 0.0 copy-start.3
  116.0 1.0 copy-done.3
  117.0 127.8 %attn.1 = (bf16[512,4096]{1,0:T(8,128)(2,1)}, bf16[512,4096]{1,0:T(8,128)(2,1)}) custom-call(s32[2]{0:T(128)} %pad_add_fusion.meta, bf16[32,1024,128]{2,1,0:T(8,128)(2,1)} %q_proj.1.q_ref, bf16[2,4,512,128]{3,2,1,0:T(8,128)(2,1)} %get-tuple-element.9.own_hbm, bf16[2,4,512,128]{3,2,1,0:T(8,128)(2,1)} %copy-done.2, bf16[2,4,512,128]{3,2,1,0:T(8,128)(2,1)} %copy-done.4, ...), custom_call_target="tpu_custom_call" | custom-call | flops 34359738368 | bytes 25165824 | tf_op jit(solution)/shard_map/attn/pallas_call | solution.py:228
  244.8 0.5 collective-permute-start.4
  245.3 6.8 %collective-permute-done.4.recv_ref = bf16[512,4096]{1,0:T(8,128)(2,1)} collective-permute-done((bf16[512,4096]{1,0:T(8,128)(2,1)}, bf16[512,4096]{1,0:T(8,128)(2,1)}, u32[]{:S(2)}, u32[]{:S(2)}) %collective-permute-start.4) | collective-permute-done | bytes 4194336 | tf_op jit(solution)/shard_map/ppermute | solution.py:299
  252.1 53.7 %out_proj.1 = bf16[512,5120]{1,0:T(8,128)(2,1)} custom-call(s32[1]{0:T(128)} %bitcast.meta, bf16[512,4096]{1,0:T(8,128)(2,1)} %get-tuple-element.11.keep_ref, bf16[512,4096]{1,0:T(8,128)(2,1)} %collective-permute-done.4.recv_ref, bf16[8192,5120]{1,0:T(8,128)(2,1)} %wb_ref.1, bf16[8192,5120]{1,0:T(8,128)(2,1)} %wb_ref.1, bf16[512,5120]{1,0:T(8,128)(2,1)} %x_ref.1), custom_call_target="tpu_custom_call" | custom-call | flops 42949672960 | bytes 83886080 | tf_op jit(solution)/shard_map/out_proj/pallas_call | solution.py:264
  (6 shorter events, 0.0 us)
Async XLA Ops:
  0.0 11.8 %copy-start = (bf16[128]{0:T(256)(128)(2,1)S(1)}, bf16[128]{0:T(256)(128)(2,1)}, u32[]{:S(2)}) copy-start(bf16[128]{0:T(256)(128)(2,1)} %param.15) | copy-start | bytes 772
  11.1 28.7 %collective-permute-start = (bf16[512,5120]{1,0:T(8,128)(2,1)}, bf16[512,5120]{1,0:T(8,128)(2,1)}, u32[]{:S(2)}, u32[]{:S(2)}) collective-permute-start(bf16[512,5120]{1,0:T(8,128)(2,1)} %fusion.2.own_hbm.h_ref), channel_id=1, source_target_pairs={{0,1},{1,0},{2,3},{3,2},{4,5},{5,4},{6,7},{7,6}} | collective-permute-start | bytes 15728648 | tf_op jit(solution)/shard_map/ppermute | solution.py:290
  14.0 21.8 %copy-start.1 = (bf16[128]{0:T(256)(128)(2,1)S(1)}, bf16[128]{0:T(256)(128)(2,1)}, u32[]{:S(2)}) copy-start(bf16[128]{0:T(256)(128)(2,1)} %param.14) | copy-start | bytes 772
  32.9 81.8 %collective-permute-start.1 = (bf16[2,4,512,128]{3,2,1,0:T(8,128)(2,1)}, bf16[2,4,512,128]{3,2,1,0:T(8,128)(2,1)S(1)}, u32[]{:S(2)}, u32[]{:S(2)}) collective-permute-start(bf16[2,4,512,128]{3,2,1,0:T(8,128)(2,1)} %get-tuple-element.10), channel_id=1, source_target_pairs={{0,1},{1,0},{2,3},{3,2},{4,5},{5,4},{6,7},{7,6}} | collective-permute-start | bytes 3145736 | tf_op jit(solution)/shard_map/ppermute | solution.py:294
  33.0 81.8 %collective-permute-start.3 = (bf16[2,4,512,128]{3,2,1,0:T(8,128)(2,1)}, bf16[2,4,512,128]{3,2,1,0:T(8,128)(2,1)S(1)}, u32[]{:S(2)}, u32[]{:S(2)}) collective-permute-start(bf16[2,4,512,128]{3,2,1,0:T(8,128)(2,1)} %get-tuple-element.10), channel_id=1, source_target_pairs={{0,3},{1,2},{4,7},{5,6}} | collective-permute-start | bytes 3145736 | tf_op jit(solution)/shard_map/ppermute | solution.py:296
  34.3 80.5 %collective-permute-start.2 = (bf16[2,4,512,128]{3,2,1,0:T(8,128)(2,1)}, bf16[2,4,512,128]{3,2,1,0:T(8,128)(2,1)S(1)}, u32[]{:S(2)}, u32[]{:S(2)}) collective-permute-start(bf16[2,4,512,128]{3,2,1,0:T(8,128)(2,1)} %get-tuple-element.9.own_hbm), channel_id=1, source_target_pairs={{0,2},{1,3},{4,6},{5,7}} | collective-permute-start | bytes 3145736 | tf_op jit(solution)/shard_map/ppermute | solution.py:295
  114.7 1.0 copy-start.2
  114.7 1.3 copy-start.4
  116.0 1.0 copy-start.3
  244.8 7.3 %collective-permute-start.4 = (bf16[512,4096]{1,0:T(8,128)(2,1)}, bf16[512,4096]{1,0:T(8,128)(2,1)}, u32[]{:S(2)}, u32[]{:S(2)}) collective-permute-start(bf16[512,4096]{1,0:T(8,128)(2,1)} %get-tuple-element.12), channel_id=1, source_target_pairs={{0,1},{1,0},{2,3},{3,2},{4,5},{5,4},{6,7},{7,6}} | collective-permute-start | bytes 12582920 | tf_op jit(solution)/shard_map/ppermute | solution.py:299
